TPU v7x, 32 devices: a whole 2x2x4 slice. The times are simulated.
32 devices in a mesh: blk: 8 (over y, x, core), grp: 4 (over z).
Axes of the slice: x: 2, y: 2, z: 4, core: 2. Of those that a mesh axis runs over, the one named last changes fastest.
Arguments:
- samples: float32 [32, 128, 256], P('blk', 'grp'), may hold values from -11 to 11
- pair_table: int32 [32, 16], P('blk'), may hold values from 0 to 31
- assignment: int32 [2, 32], P(None, 'blk'), may hold values from 0 to 127
- band_index: int32 [2], replicated, may hold values from 0 to 1023
Outputs:
- log_weight: float32 [2, 32, 128], P(None, 'blk', 'grp')
All inputs are finite; a program needn't handle non-finite values.
Results may differ from a plain program's by a relative error of at most 0.0003.
Values sent between devices are 32-bit elements; how exact they have to be, the bound alone decides.
No kernel may reach another device: no remote copies, remote signals or barrier semaphores. Data moves between devices by JAX's collectives and lax.ppermute only.
A program may use at most 128 MiB of HBM per device.

v0:
```python
import jax
import jax.numpy as jnp
from jax import lax
from jax.sharding import PartitionSpec as P

PAIRS = 16


def joined_2(shard, axis, combine):
    everything = jax.tree.map(lambda part: lax.all_gather(part, axis), shard)
    initial = jax.tree.map(lambda part: part[0], everything)

    def hop(k, so_far):
        return combine(so_far, jax.tree.map(lambda part: part[k], everything))

    return lax.fori_loop(1, lax.axis_size(axis), hop, initial)


def make_fold(queries, query_norm, band_list, counts):

    def fold(state, shard_rows, offset):
        count_in = shard_rows.shape[0]
        rows_dev = shard_rows.shape[1]

        def compute(inner):
            key_rows = shard_rows.reshape(count_in * rows_dev, shard_rows.shape[2])
            key_norm = jnp.sum(key_rows * key_rows, -1)
            product = jnp.einsum("qd,kd->qk", queries, key_rows, precision=lax.Precision.HIGHEST)
            distance = query_norm[:, None] + key_norm[None, :] - 2.0 * product
            blocks = []
            for band_sq in band_list:
                scores = (-distance / (2.0 * band_sq)).reshape(
                    distance.shape[0], count_in, rows_dev
                )
                peak = jnp.max(scores, -1)
                blocks.append(peak + jnp.log(jnp.sum(jnp.exp(scores - peak[..., None]), -1)))
            update = jnp.stack(blocks)
            return lax.dynamic_update_slice(inner, update, (0, 0, offset))

        needed = jnp.any(counts > 0)
        return lax.cond(needed, compute, lambda inner: inner, state)

    return fold


def per_device(samples, pair_table, assignment, band_index):
    local_subs, rows_dev, width = samples.shape
    rounds = assignment.shape[0]
    group_size = lax.axis_size("grp")
    group_index = lax.axis_index("grp")
    members = local_subs * lax.axis_size("blk")
    band_sq = width * (1.0 + band_index.astype(jnp.float32) / 256.0) / 32.0
    local_pick = assignment - group_index * rows_dev
    onehot = (
        local_pick[:, :, None] == jnp.arange(rows_dev, dtype=jnp.int32)[None, None, :]
    ).astype(jnp.float32)
    picked = jnp.einsum("tsr,srd->td", onehot, samples, precision=lax.Precision.HIGHEST)
    centre = lax.psum(picked, ("blk", "grp")) / members
    member_ids = jnp.arange(members, dtype=jnp.int32)
    count_int = jnp.sum(
        (pair_table[:, :, None] == member_ids[None, None, :]).astype(jnp.int32), axis=1
    )
    counts = count_int.astype(jnp.float32)
    gathered = lax.all_gather(samples, "grp", axis=1, tiled=True)
    query_count = local_subs * rows_dev * group_size
    queries = gathered.reshape(query_count, width)
    query_norm = jnp.sum(queries * queries, -1)
    start_state = jnp.zeros((rounds, query_count, members), jnp.float32)
    fold = make_fold(queries, query_norm, [band_sq[turn] for turn in range(rounds)], count_int)
    partial_value = fold(
        start_state, lax.all_gather(samples, "blk", axis=0, tiled=True), jnp.int32(0)
    )
    split_view = partial_value.reshape(rounds, local_subs, group_size, rows_dev, members)
    swapped = lax.all_to_all(split_view, "grp", split_axis=2, concat_axis=2, tiled=True)
    peak = jnp.max(swapped, 2)
    kernel = peak + jnp.log(jnp.sum(jnp.exp(swapped - peak[:, :, None]), 2))
    weighted = jnp.einsum("tsrm,sm->tsr", kernel, counts, precision=lax.Precision.HIGHEST) / PAIRS
    spread = samples[None] - centre[:, None, None, :]
    logits = weighted - jnp.sum(spread * spread, -1) / (2.0 * band_sq[:, None, None])
    row_peak = jnp.max(logits, -1)
    row_total = jnp.sum(jnp.exp(logits - row_peak[..., None]), -1)

    def combine_pair(first, second):
        joined = jnp.maximum(first[0], second[0])
        return (
            joined,
            first[1] * jnp.exp(first[0] - joined) + second[1] * jnp.exp(second[0] - joined),
        )

    peak_all, total_all = joined_2((row_peak, row_total), "grp", combine_pair)
    return logits - peak_all[..., None] - jnp.log(total_all)[..., None]


def solution(mesh):
    return jax.shard_map(
        per_device,
        mesh=mesh,
        in_specs=(P("blk", "grp", None), P("blk", None), P(None, "blk"), P()),
        out_specs=P(None, "blk", "grp"),
        check_vma=False,
    )
```

profile of v0, /device:TPU:0, one launch (start us, length us, event | category | flops | bytes accessed | tf_op | source)
XLA Modules:
  0.0 123.1 jit_solution(9642932200936565193)
XLA Ops:
  6.5 0.7 all-gather.6.cloned.1.call-update
  7.3 0.8 convert_reduce_fusion
  8.0 0.6 compare_reduce_fusion
  9.3 0.7 broadcast_subtract_fusion
  10.1 1.2 convolution_bitcast_fusion
  11.3 42.0 %psum.7 = f32[2,256]{1,0:T(2,128)S(1)} all-reduce(f32[2,256]{1,0:T(2,128)S(1)} %convolution_bitcast_fusion), channel_id=1, replica_groups=mesh['blk'=8,'grp'=4] {'blk','grp'}, use_global_device_ids=true, to_apply=%region_12.0 | all-reduce | flops 512 | bytes 4096 | tf_op jit(solution)/shard_map/psum | solution.py:58
  53.2 15.9 %all_gather.18 = f32[4,128,256]{2,1,0:T(8,128)S(1)} all-gather(f32[4,32,256]{2,1,0:T(8,128)} %param.8), channel_id=1, replica_groups=mesh['blk'=8,'grp'=4] {'grp'}, dimensions={1}, use_global_device_ids=true | all-gather | bytes 655360 | tf_op jit(solution)/shard_map/all_gather | solution.py:64
  69.2 0.7 multiply_add_fusion
  69.8 14.7 %conditional.1 = (f32[2,512,32]{1,2,0:T(8,128)S(1)}) conditional(s32[]{:T(128)} %convert_element_type.15, () %tuple.36, (f32[4,128,256]{2,1,0:T(8,128)S(1)}, f32[32,32,256]{2,1,0:T(8,128)}, f32[2]{0:T(128)S(1)}) %tuple.37), branch_computations={%region_2.0_spmd, %region_3.10_spmd} | conditional | flops 1617689088 | bytes 25186376 | solution.py:41
  69.8 1.4 %multiply_reduce_fusion = f32[32,32]{1,0:T(8,128)S(1)} fusion(f32[32,32,256]{2,1,0:T(8,128)} %get-tuple-element.164), kind=kLoop, calls=%fused_computation.11 | loop fusion | flops 523264 | bytes 1052672 | tf_op jit(solution)/shard_map/cond/branch_1_fun/reduce_sum | solution.py:27
  71.3 0.7 fusion.12
  73.5 5.3 %broadcast_divide_fusion.1 = (f32[512,1024]{1,0:T(8,128)}, f32[512,1024]{1,0:T(8,128)}) fusion(f32[]{:T(128)} %bitcast.3, f32[]{:T(128)} %bitcast.6, f32[512,256]{1,0:T(8,128)S(1)} %bitcast.71, f32[1024,256]{1,0:T(8,128)} %bitcast.74, f32[1024]{0:T(1024)S(1)} %add.87, f32[512]{0:T(512)S(1)} %bitcast.80), kind=kOutput, calls=%fused_computation.10 | convolution fusion | flops 1613758464 | bytes 5773320 | tf_op jit(solution)/shard_map/cond/branch_1_fun/qd,kd->qk/dot_general | solution.py:28
  78.8 1.9 %copy.16 = f32[512,1024]{0,1:T(8,128)S(1)} copy(f32[512,1024]{1,0:T(8,128)} %get-tuple-element.190) | data formatting | bytes 4194304 | tf_op jit(solution)/shard_map/cond/branch_1_fun/div | solution.py:32
  81.1 0.5 fusion.3
  81.6 1.9 %copy.17 = f32[512,1024]{0,1:T(8,128)S(1)} copy(f32[512,1024]{1,0:T(8,128)} %get-tuple-element.191) | data formatting | bytes 4194304 | tf_op jit(solution)/shard_map/cond/branch_1_fun/div | solution.py:32
  83.9 0.5 fusion.1
  84.9 1.0 reshape.97
  85.9 3.8 %all-to-all-start = ((f32[4,1,8192]{2,1,0:T(1,128)}), f32[4,1,8192]{2,1,0:T(1,128)S(1)}, u32[]{:S(2)}, u32[]{:S(2)}) async-start(f32[4,1,8192]{2,1,0:T(1,128)} %reshape.97), calls=%async_computation | async-start | bytes 262144 | tf_op jit(solution)/shard_map/all_to_all | solution.py:74
  89.8 5.8 %all-to-all-done = f32[4,1,8192]{2,1,0:T(1,128)S(1)} async-done(((f32[4,1,8192]{2,1,0:T(1,128)}), f32[4,1,8192]{2,1,0:T(1,128)S(1)}, u32[]{:S(2)}, u32[]{:S(2)}) %all-to-all-start) | async-done | bytes 131104 | tf_op jit(solution)/shard_map/all_to_all | solution.py:74
  95.6 0.5 broadcast.44
  96.1 1.0 reduce.5
  98.3 9.0 %all-gather.3 = f32[4,2,4]{2,1,0:T(2,128)S(1)} all-gather(f32[1,2,4]{2,1,0:T(2,128)S(1)} %bitcast.79), channel_id=3, replica_groups=mesh['blk'=8,'grp'=4] {'grp'}, dimensions={0}, use_global_device_ids=true | all-gather | bytes 160 | tf_op jit(solution)/shard_map/all_gather | solution.py:10
  107.3 8.2 %all-gather.2 = f32[4,2,4]{2,1,0:T(2,128)S(1)} all-gather(f32[1,2,4]{2,1,0:T(2,128)S(1)} %bitcast.77), channel_id=2, replica_groups=mesh['blk'=8,'grp'=4] {'grp'}, dimensions={0}, use_global_device_ids=true | all-gather | bytes 160 | tf_op jit(solution)/shard_map/all_gather | solution.py:10
  115.6 0.7 subtract_subtract_fusion
  (31 shorter events, 2.9 us)
Async XLA Ops:
  6.5 63.3 %all-gather.6.cloned.1.call-start = ((), (), s32[]{:S(2)}) async-start(), calls=%async_computation.1 | async-start | bytes 1179648 | tf_op jit(solution)/shard_map/all_gather | solution.py:71
  84.5 5.2 %copy-start = (f32[4,32,256]{2,1,0:T(8,128)S(1)}, f32[4,32,256]{2,1,0:T(8,128)}, u32[]{:S(2)}) copy-start(f32[4,32,256]{2,1,0:T(8,128)} %param.8) | copy-start | bytes 393220
  85.9 9.7 %all-to-all-start = ((f32[4,1,8192]{2,1,0:T(1,128)}), f32[4,1,8192]{2,1,0:T(1,128)S(1)}, u32[]{:S(2)}, u32[]{:S(2)}) async-start(f32[4,1,8192]{2,1,0:T(1,128)} %reshape.97), calls=%async_computation | async-start | bytes 262144 | tf_op jit(solution)/shard_map/all_to_all | solution.py:74
Sparse Core Ops, SparseCore 0:
  9.2 26.2 all-gather.5
where the time goes:
time: 124 us; the launch traced here: 123 us
  blocking collectives  75 us (60%)
  between operations  14.1 us (11%)
  other arithmetic  8.66 us (7%)
  local copies, waits for them, and re-layouts  6.86 us (6%)
  matrix products  6.7 us (5%)
  waiting for transfers between devices  6.5 us (5%)
  starting transfers between devices  3.8 us (3%)
  loops' own time  1.43 us (1%)
    psum x1, blocking collectives, per_device(): centre = lax.psum(picked, ('blk', 'grp')) / members  42 us
    all_gather x2, blocking collectives, joined_2(): everything = jax.tree.map(lambda part: lax.all_gather(part, axis), shard)  17.2 us
    all_gather x1, blocking collectives, per_device(): gathered = lax.all_gather(samples, 'grp', axis=1, tiled=True)  15.9 us
    all_to_all x1, waiting for transfers between devices, per_device(): lax.all_to_all(split_view, 'grp', split_axis=2, concat_axis=2, tiled=True)  5.79 us
    dot_general x1, matrix products, compute(): jnp.einsum('qd,kd->qk', queries, key_rows, precision=lax.Precision.HIGHEST)  5.35 us
    div x2, local copies, waits for them, and re-layouts, compute(): -distance / (2.0 * band_sq)  3.84 us
    all_to_all x1, starting transfers between devices, per_device(): lax.all_to_all(split_view, 'grp', split_axis=2, concat_axis=2, tiled=True)  3.8 us
  transfers between devices with their start and end apart: 2, of which 1 were waited for; matrix products, arithmetic and copies ran while one was open for 3% of the time, Pallas kernels for 0%

commit v1 on v0

--- a/solution.py
+++ b/solution.py
@@ -61,7 +61,9 @@
         (pair_table[:, :, None] == member_ids[None, None, :]).astype(jnp.int32), axis=1
     )
     counts = count_int.astype(jnp.float32)
-    gathered = lax.all_gather(samples, "grp", axis=1, tiled=True)
+    gathered = jnp.concatenate(
+        lax.all_to_all(jnp.stack([samples] * lax.axis_size("grp")), "grp", 0, 0), axis=1
+    )
     query_count = local_subs * rows_dev * group_size
     queries = gathered.reshape(query_count, width)
     query_norm = jnp.sum(queries * queries, -1)

time: 124 us -> 113 us (0.911)
  blocking collectives: 75 us -> 57.9 us
  starting transfers between devices: 3.8 us -> 9.9 us
  local copies, waits for them, and re-layouts: 6.86 us -> 8.7 us
    all_gather x1 -> x0, blocking collectives: 15.9 us -> none  [per_device(): gathered = lax.all_gather(samples, 'grp', axis=1, tiled=True)]
    all_to_all x0 -> x1, starting transfers between devices: none -> 6.35 us  [per_device(): lax.all_to_all(jnp.stack([samples] * lax.axis_size('grp')), 'grp', 0, 0)]
    another operation x0 -> x1, local copies, waits for them, and re-layouts: none -> 1.75 us  [per_device(): jnp.stack([samples] * lax.axis_size('grp'))]
  transfers between devices with their start and end apart: 2 -> 3, of which waited for: 1 -> 1; matrix products, arithmetic and copies ran while one was open for 3% -> 5% of each run, Pallas kernels for 0% -> 0%
where the time goes in v1:
time: 113 us
  blocking collectives  57.9 us (51%)
  between operations  14.1 us (12%)
  starting transfers between devices  9.9 us (9%)
  other arithmetic  8.73 us (8%)
  local copies, waits for them, and re-layouts  8.7 us (8%)
  waiting for transfers between devices  6.5 us (6%)
  matrix products  5.48 us (5%)
  loops' own time  1.46 us (1%)
    psum x1, blocking collectives, per_device(): centre = lax.psum(picked, ('blk', 'grp')) / members  40.8 us
    all_gather x2, blocking collectives, joined_2(): everything = jax.tree.map(lambda part: lax.all_gather(part, axis), shard)  17.2 us
    all_to_all x1, starting transfers between devices, per_device(): lax.all_to_all(jnp.stack([samples] * lax.axis_size('grp')), 'grp', 0, 0)  6.35 us
    all_to_all x1, waiting for transfers between devices, per_device(): lax.all_to_all(split_view, 'grp', split_axis=2, concat_axis=2, tiled=True)  5.79 us
    dot_general x1, matrix products, compute(): jnp.einsum('qd,kd->qk', queries, key_rows, precision=lax.Precision.HIGHEST)  4.13 us
    div x2, local copies, waits for them, and re-layouts, compute(): -distance / (2.0 * band_sq)  3.84 us
    all_to_all x1, starting transfers between devices, per_device(): lax.all_to_all(split_view, 'grp', split_axis=2, concat_axis=2, tiled=True)  3.55 us
  transfers between devices with their start and end apart: 3, of which 1 were waited for; matrix products, arithmetic and copies ran while one was open for 5% of the time, Pallas kernels for 0%

profile of v1, /device:TPU:0, one launch (start us, length us, event | category | flops | bytes accessed | tf_op | source)
XLA Modules:
  0.0 112.8 jit_solution(1516808820120411792)
XLA Ops:
  6.5 0.7 all-gather.6.cloned.1.call-update
  7.3 1.7 %stack.5 = f32[4,4,32,256]{3,2,1,0:T(8,128)} broadcast(f32[4,32,256]{2,1,0:T(8,128)} %param.8), dimensions={1,2,3} | broadcast | bytes 655360 | tf_op jit(solution)/shard_map/stack | solution.py:65
  9.0 6.3 %all-to-all-start = ((f32[4,4,32,256]{3,2,1,0:T(8,128)}), f32[4,4,32,256]{3,2,1,0:T(8,128)S(1)}, u32[]{:S(2)}, u32[]{:S(2)}) async-start(f32[4,4,32,256]{3,2,1,0:T(8,128)} %stack.5), calls=%async_computation | async-start | bytes 1048576 | tf_op jit(solution)/shard_map/all_to_all | solution.py:65
  15.3 0.8 convert_reduce_fusion
  16.1 0.6 compare_reduce_fusion
  17.4 0.7 broadcast_subtract_fusion
  18.2 1.2 %convolution_bitcast_fusion = f32[2,256]{1,0:T(2,128)S(1)} fusion(f32[4,32,256]{2,1,0:T(8,128)} %param.8, s32[2,4]{0,1:T(4,128)S(1)} %copy.22), kind=kOutput, calls=%fused_computation.22 | convolution fusion | flops 786688 | bytes 133152 | tf_op jit(solution)/shard_map/tsr,srd->td/dot_general | solution.py:57
  19.4 40.8 %psum.7 = f32[2,256]{1,0:T(2,128)S(1)} all-reduce(f32[2,256]{1,0:T(2,128)S(1)} %convolution_bitcast_fusion), channel_id=1, replica_groups=mesh['blk'=8,'grp'=4] {'blk','grp'}, use_global_device_ids=true, to_apply=%region_12.0 | all-reduce | flops 512 | bytes 4096 | tf_op jit(solution)/shard_map/psum | solution.py:58
  60.1 0.7 multiply_add_fusion
  60.8 13.6 %conditional.1 = (f32[2,512,32]{1,2,0:T(8,128)S(1)}) conditional(s32[]{:T(128)} %convert_element_type.15, () %tuple.36, (f32[4,4,32,256]{3,2,0,1:T(8,128)S(1)}, f32[32,32,256]{2,1,0:T(8,128)}, f32[2]{0:T(128)S(1)}) %tuple.66), branch_computations={%region_2.0_spmd, %region_3.10_spmd} | conditional | flops 1617689088 | bytes 29909092 | solution.py:41
  61.1 1.5 %multiply_reduce_fusion = f32[32,32]{1,0:T(8,128)S(1)} fusion(f32[32,32,256]{2,1,0:T(8,128)} %get-tuple-element.164), kind=kLoop, calls=%fused_computation.11 | loop fusion | flops 523264 | bytes 1052672 | tf_op jit(solution)/shard_map/cond/branch_1_fun/reduce_sum | solution.py:27
  62.7 0.7 fusion.12
  64.7 4.1 %broadcast_divide_fusion.1 = (f32[512,1024]{1,0:T(8,128)}, f32[512,1024]{1,0:T(8,128)}) fusion(f32[]{:T(128)} %bitcast.2, f32[]{:T(128)} %bitcast.5, f32[512,256]{1,0:T(8,128)S(1)} %bitcast.76, f32[1024,256]{1,0:T(8,128)S(1)} %bitcast.74, f32[1024]{0:T(1024)S(1)} %add.87, f32[512]{0:T(512)S(1)} %reduce_sum.68), kind=kOutput, calls=%fused_computation.10 | convolution fusion | flops 1613758464 | bytes 5773320 | tf_op jit(solution)/shard_map/cond/branch_1_fun/qd,kd->qk/dot_general | solution.py:28
  68.8 1.9 %copy.18 = f32[512,1024]{0,1:T(8,128)S(1)} copy(f32[512,1024]{1,0:T(8,128)} %get-tuple-element.199) | data formatting | bytes 4194304 | tf_op jit(solution)/shard_map/cond/branch_1_fun/div | solution.py:32
  71.6 1.9 %copy.19 = f32[512,1024]{0,1:T(8,128)S(1)} copy(f32[512,1024]{1,0:T(8,128)} %get-tuple-element.200) | data formatting | bytes 4194304 | tf_op jit(solution)/shard_map/cond/branch_1_fun/div | solution.py:32
  73.9 0.5 fusion.1
  74.9 1.0 reshape.98
  75.9 3.6 %all-to-all-start.1 = ((f32[4,1,8192]{2,1,0:T(1,128)}), f32[4,1,8192]{2,1,0:T(1,128)S(1)}, u32[]{:S(2)}, u32[]{:S(2)}) async-start(f32[4,1,8192]{2,1,0:T(1,128)} %reshape.98), calls=%async_computation.1 | async-start | bytes 262144 | tf_op jit(solution)/shard_map/all_to_all | solution.py:76
  79.5 5.8 %all-to-all-done.1 = f32[4,1,8192]{2,1,0:T(1,128)S(1)} async-done(((f32[4,1,8192]{2,1,0:T(1,128)}), f32[4,1,8192]{2,1,0:T(1,128)S(1)}, u32[]{:S(2)}, u32[]{:S(2)}) %all-to-all-start.1) | async-done | bytes 131104 | tf_op jit(solution)/shard_map/all_to_all | solution.py:76
  85.3 0.5 broadcast.46
  85.8 1.0 reduce.5
  88.0 9.0 %all-gather.3 = f32[4,2,4]{2,1,0:T(2,128)S(1)} all-gather(f32[1,2,4]{2,1,0:T(2,128)S(1)} %bitcast.80), channel_id=3, replica_groups=mesh['blk'=8,'grp'=4] {'grp'}, dimensions={0}, use_global_device_ids=true | all-gather | bytes 160 | tf_op jit(solution)/shard_map/all_gather | solution.py:10
  97.0 8.2 %all-gather.2 = f32[4,2,4]{2,1,0:T(2,128)S(1)} all-gather(f32[1,2,4]{2,1,0:T(2,128)S(1)} %bitcast.78), channel_id=2, replica_groups=mesh['blk'=8,'grp'=4] {'grp'}, dimensions={0}, use_global_device_ids=true | all-gather | bytes 160 | tf_op jit(solution)/shard_map/all_gather | solution.py:10
  105.3 0.7 subtract_subtract_fusion
  (36 shorter events, 3.6 us)
Async XLA Ops:
  6.5 54.3 %all-gather.6.cloned.1.call-start = ((), (), s32[]{:S(2)}) async-start(), calls=%async_computation.2 | async-start | bytes 1179648 | tf_op jit(solution)/shard_map/all_gather | solution.py:73
  9.0 51.8 %all-to-all-start = ((f32[4,4,32,256]{3,2,1,0:T(8,128)}), f32[4,4,32,256]{3,2,1,0:T(8,128)S(1)}, u32[]{:S(2)}, u32[]{:S(2)}) async-start(f32[4,4,32,256]{3,2,1,0:T(8,128)} %stack.5), calls=%async_computation | async-start | bytes 1048576 | tf_op jit(solution)/shard_map/all_to_all | solution.py:65
  60.8 3.8 %copy-start.1 = (f32[32,32,256]{2,1,0:T(8,128)S(1)}, f32[32,32,256]{2,1,0:T(8,128)}, u32[]{:S(2)}) copy-start(f32[32,32,256]{2,1,0:T(8,128)} %get-tuple-element.164) | copy-start | bytes 3145732 | tf_op jit(solution)/shard_map/cond
  74.4 5.0 %copy-start = (f32[4,32,256]{2,1,0:T(8,128)S(1)}, f32[4,32,256]{2,1,0:T(8,128)}, u32[]{:S(2)}) copy-start(f32[4,32,256]{2,1,0:T(8,128)} %param.8) | copy-start | bytes 393220
  75.9 9.5 %all-to-all-start.1 = ((f32[4,1,8192]{2,1,0:T(1,128)}), f32[4,1,8192]{2,1,0:T(1,128)S(1)}, u32[]{:S(2)}, u32[]{:S(2)}) async-start(f32[4,1,8192]{2,1,0:T(1,128)} %reshape.98), calls=%async_computation.1 | async-start | bytes 262144 | tf_op jit(solution)/shard_map/all_to_all | solution.py:76
Sparse Core Ops, SparseCore 0:
  9.2 26.1 all-gather.5
